TPU v7x, 512 devices: a whole 4x4x16 slice. The times are simulated.
512 devices in a mesh: dp: 32 (over y, z_lo), mp: 16 (over x, z_hi, core).
Axes of the slice: x: 4, y: 4, z: 16 (z_hi: 2, z_lo: 8; z = z_hi * 8 + z_lo), core: 2. Of those that a mesh axis runs over, the one named last changes fastest.
Arguments:
- logits: bfloat16 [4096, 65536], P('dp', 'mp'), may hold values from -72 to 240
- targets: int32 [4096], P('dp'), may hold values from 0 to 65535
- resp_mask: int32 [4096], P('dp'), may hold values from 0 to 1, as said below
- rewards: int32 [32], P('dp'), may hold values from 0 to 10
- groups: int32 [32], P('dp'), may hold values from 0 to 7, as said below
- unit_grad: bfloat16 [4096, 8192], P(('dp', 'mp')), may hold values from -192 to 192
- mix: bfloat16 [4096, 8192], P('dp', 'mp'), may hold values from -6 to 6
- w_out: bfloat16 [8192, 8192], P('mp', 'dp'), may hold values from -0.0625 to 0.0625
Outputs:
- token_logprob: float32 [4096], P('dp')
- policy_loss: float32 [], replicated
- grad_mix: bfloat16 [4096, 8192], P('dp', 'mp')
- grad_w_out: bfloat16 [8192, 8192], P('mp', 'dp')
Inputs may be any that keep to these rules, and one draw needn't show every extreme that they name: `resp_mask`: in each sample the response mask is a run of ones followed by zeros, with at least 32 ones. `groups`: each prompt id names exactly 4 samples.
All inputs are finite; a program needn't handle non-finite values.
Results may differ from a plain program's by a relative error of at most 0.005.
Values may be sent and summed in bfloat16 or wider, within the bound.
A program may use at most 64 MiB of HBM per device.

v0:
```python
import jax
import jax.numpy as jnp
from jax import lax
from jax.sharding import Mesh
from jax.sharding import PartitionSpec as P

K = 4
DP = ("dp_0", "dp_1")
DP_MP = ("dp_0", "dp_1", "mp")


def from_everyone(shard, axis):
    count = lax.axis_size(axis)
    return lax.all_to_all(
        jnp.broadcast_to(shard[None], (count, *shard.shape)), axis, 0, 0, tiled=True
    )


def collected_together(shard, axis):
    leaves = jax.tree.leaves(shard)
    sequence = sorted(range(len(leaves)), key=lambda k: -leaves[k].size)
    width = (1, *leaves[sequence[0]].shape)[-1]
    lines = [
        jnp.pad(leaves[k].reshape(-1), (0, -leaves[k].size % width)).reshape(-1, width)
        for k in sequence
    ]
    both, at, found = (from_everyone(jnp.concatenate(lines), axis), 0, {})
    for k, line in zip(sequence, lines):
        piece = both[:, at : at + len(line)].reshape(len(both), -1)
        found[k] = piece[:, : leaves[k].size].reshape(-1, *leaves[k].shape)
        at += len(line)
    numbers = iter(range(len(leaves)))
    return jax.tree.map(lambda _: found[next(numbers)], shard)


def joined_by_halves(pieces, combine):
    while len(jax.tree.leaves(pieces)[0]) > 1:
        pieces = jax.vmap(combine)(
            *(jax.tree.map(lambda part: part[side::2], pieces) for side in (0, 1))
        )
    return jax.tree.map(lambda part: part[0], pieces)


def merged(shard, axis, combine):
    pieces = collected_together(shard, axis)
    return joined_by_halves(pieces, combine)


def of_everyone(shard, axis):
    everything = from_everyone(shard, axis)
    return jnp.sum(everything, axis=0)


def packed_total(arrays, axis):
    vector, at, gathered = (jnp.concatenate([a.reshape(-1) for a in arrays]), 0, [])
    total = of_everyone(vector, axis)
    for a in arrays:
        gathered.append(total[at : at + a.size].reshape(a.shape))
        at += a.size
    return tuple(gathered)


def whole_of(shard, axes, dim):
    for axis in reversed(axes):
        shard = lax.all_gather(shard, axis, axis=dim, tiled=True)
    return shard


def merge_stats(first, second):
    highest = jnp.maximum(first[0], second[0])
    summed = first[1] * jnp.exp(first[0] - highest) + second[1] * jnp.exp(second[0] - highest)
    return (highest, summed, first[2] + second[2])


def shards(logits, targets, resp_mask, rewards, groups, unit_grad, mix, w_out):
    tok_rows, vocab_dev = logits.shape
    mp_lane = lax.axis_index("mp")
    local_target = targets - mp_lane * vocab_dev
    present = (local_target >= 0) & (local_target < vocab_dev)
    picked = jnp.take_along_axis(logits, jnp.clip(local_target, 0, vocab_dev - 1)[:, None], axis=1)[
        :, 0
    ]
    picked = jnp.where(present, picked.astype(jnp.float32), 0.0)
    local_max = jnp.max(logits, axis=1).astype(jnp.float32)
    local_sum = jnp.sum(jnp.exp(logits.astype(jnp.float32) - local_max[:, None]), axis=1)
    highest, summed, target_logit = merged((local_max, local_sum, picked), "mp", merge_stats)
    logprob = target_logit - (highest + jnp.log(summed))
    mask_float = resp_mask.astype(jnp.float32)
    local_count = jnp.sum(mask_float)
    reward_float = rewards.astype(jnp.float32)
    prompt_slots = jnp.arange(lax.axis_size(DP) // K, dtype=jnp.int32)
    own_slot = (prompt_slots == groups[0]).astype(jnp.float32)
    group_total, token_count = packed_total((own_slot * reward_float[0], local_count), DP)
    own_total = jnp.sum(own_slot * group_total)
    advantage = reward_float[0] - (own_total - reward_float[0]) / (K - 1)
    weight = advantage * mask_float / token_count
    policy_loss = of_everyone(-jnp.sum(weight * logprob), DP)
    sub_rows = unit_grad.shape[0]
    part_weight = lax.dynamic_slice_in_dim(weight, mp_lane * sub_rows, sub_rows)
    grad_local = (-part_weight[:, None] * unit_grad.astype(jnp.float32)).astype(jnp.bfloat16)
    grad_group = lax.all_gather(grad_local, "mp", axis=0, tiled=True)
    grad_mix = lax.dot_general(
        grad_group,
        whole_of(w_out, DP, 1),
        (((1,), (1,)), ((), ())),
        preferred_element_type=jnp.float32,
    ).astype(jnp.bfloat16)
    grad_every = lax.all_to_all(grad_group, DP, split_axis=1, concat_axis=0, tiled=True)
    grad_w_out = lax.dot_general(
        lax.all_gather(mix, DP, axis=0, tiled=True),
        grad_every,
        (((0,), (0,)), ((), ())),
        preferred_element_type=jnp.float32,
    ).astype(jnp.bfloat16)
    return (logprob, policy_loss, grad_mix, grad_w_out)


def solution(mesh):
    finer = Mesh(mesh.devices.reshape(4, 8, mesh.shape["mp"]), ("dp_0", "dp_1", "mp"))
    in_specs = (P(DP, "mp"), P(DP), P(DP), P(DP), P(DP), P(DP_MP, None), P(DP, "mp"), P("mp", DP))
    out_specs = (P(DP), P(), P(DP, "mp"), P("mp", DP))
    return jax.shard_map(
        shards, mesh=finer, in_specs=in_specs, out_specs=out_specs, check_vma=False
    )
```

profile of v0, /device:TPU:1, one launch (start us, length us, event | category | flops | bytes accessed | tf_op | source)
XLA Modules:
  0.0 563.2 jit_solution(692002191340332963)
XLA Ops:
  7.2 0.0 copy-start.2
  7.2 0.0 copy-start.3
  7.2 0.0 copy-start.1
  7.2 1.3 convert_reduce_fusion
  9.8 0.7 pad_maximum_fusion.1
  10.5 0.6 broadcast_in_dim.17
  11.2 16.1 %all-to-all-start.1 = ((f32[32,1,9]{2,1,0:T(1,128)}), f32[32,1,9]{2,1,0:T(1,128)S(1)}, u32[]{:S(2)}, u32[]{:S(2)}) async-start(f32[32,1,9]{2,1,0:T(1,128)} %broadcast_in_dim.17), calls=%async_computation.1 | async-start | bytes 32768 | tf_op jit(solution)/shard_map/all_to_all | solution.py:14
  27.2 0.0 all-gather.7.cloned.1.call-start
  27.3 0.7 all-gather.7.cloned.1.call-update
  28.0 0.7 fusion.5
  28.7 2.3 gather_fusion
  31.0 1.4 reduce_max.9
  32.5 1.7 exponential_reduce_fusion
  34.2 0.0 copy-done.3
  34.2 4.3 all-to-all-done.1
  38.5 0.6 broadcast_in_dim.16
  39.2 12.2 %all-to-all-start = ((f32[16,3,128]{2,1,0:T(4,128)}), f32[16,3,128]{2,1,0:T(4,128)S(1)}, u32[]{:S(2)}, u32[]{:S(2)}) async-start(f32[16,3,128]{2,1,0:T(4,128)} %broadcast_in_dim.16), calls=%async_computation | async-start | bytes 65536 | tf_op jit(solution)/shard_map/all_to_all | solution.py:14
  51.3 0.0 all-gather.5.cloned.1.call-start
  51.4 0.1 reduce_sum.56
  51.4 0.6 slice.121
  52.0 0.6 fusion.1
  53.3 12.7 %all-to-all-done = f32[16,3,128]{2,1,0:T(4,128)S(1)} async-done(((f32[16,3,128]{2,1,0:T(4,128)}), f32[16,3,128]{2,1,0:T(4,128)S(1)}, u32[]{:S(2)}, u32[]{:S(2)}) %all-to-all-start) | async-done | bytes 24608 | tf_op jit(solution)/shard_map/all_to_all | solution.py:14
  66.4 0.0 copy-done.2
  66.4 1.8 multiply_reduce_fusion
  68.2 0.1 dynamic-slice_negate_fusion
  68.2 0.0 copy-done.1
  68.2 0.7 multiply_convert_fusion
  69.0 0.0 all-gather.5.cloned.1.call-update
  69.0 0.0 all-gather.11.cloned.1.call-start
  69.1 0.7 all-gather.11.cloned.1.call-update
  69.8 0.0 all-gather.9.cloned.1.call-start
  69.8 30.2 %all-gather.7.cloned.1.call-done = bf16[512,2048]{1,0:T(8,128)(2,1)} async-done(((bf16[512,256]{1,0:T(8,128)(2,1)}), bf16[512,2048]{1,0:T(8,128)(2,1)}) %all-gather.7.cloned.1.call-update) | async-done | bytes 2097168 | tf_op jit(solution)/shard_map/all_gather | solution.py:65
  100.0 0.0 all-gather.9.cloned.1.call-update
  100.6 0.6 broadcast_in_dim.18
  101.3 9.8 %all-to-all-start.2 = ((f32[32,1,1]{2,1,0:T(1,128)}), f32[32,1,1]{2,1,0:T(1,128)S(1)}, u32[]{:S(2)}, u32[]{:S(2)}) async-start(f32[32,1,1]{2,1,0:T(1,128)} %broadcast_in_dim.18), calls=%async_computation.2 | async-start | bytes 32768 | tf_op jit(solution)/shard_map/all_to_all | solution.py:14
  111.1 83.4 %all-gather.5.cloned.1.call-done = bf16[128,8192]{1,0:T(8,128)(2,1)} async-done(((bf16[8,8192]{1,0:T(8,128)(2,1)}), bf16[128,8192]{1,0:T(8,128)(2,1)}) %all-gather.5.cloned.1.call-update) | async-done | bytes 2097168 | tf_op jit(solution)/shard_map/all_gather | solution.py:101
  194.4 4.1 copy.39
  198.5 0.0 all-to-all-done.2
  198.5 4.8 all-to-all-start.3
  203.3 0.6 reduce_sum.59
  204.0 125.4 %all-to-all-done.3 = bf16[128,32,256]{0,2,1:T(8,128)(2,1)S(1)} async-done(((bf16[128,32,256]{0,2,1:T(8,128)(2,1)}), bf16[128,32,256]{0,2,1:T(8,128)(2,1)S(1)}, u32[]{:S(2)}, u32[]{:S(2)}) %all-to-all-start.3) | async-done | bytes 2097184 | tf_op jit(solution)/shard_map/all_to_all | solution.py:108
  329.4 2.9 copy.40
  332.3 111.9 %all-gather.11.cloned.1.call-done = bf16[4096,512]{1,0:T(8,128)(2,1)} async-done(((bf16[128,512]{1,0:T(8,128)(2,1)}), bf16[4096,512]{1,0:T(8,128)(2,1)}) %all-gather.11.cloned.1.call-update) | async-done | bytes 4194320 | tf_op jit(solution)/shard_map/all_gather | solution.py:110
  444.2 4.2 fusion
  448.5 0.8 copy.41
  449.3 100.4 %all-gather.9.cloned.1.call-done = bf16[512,8192]{1,0:T(8,128)(2,1)} async-done(((bf16[512,2048]{1,0:T(8,128)(2,1)}), bf16[512,8192]{1,0:T(8,128)(2,1)}) %all-gather.9.cloned.1.call-update) | async-done | bytes 8388624 | tf_op jit(solution)/shard_map/all_gather | solution.py:65
  549.7 0.0 copy-done
  549.7 7.0 %convolution_convert_fusion.1 = bf16[128,512]{1,0:T(8,128)(2,1)} fusion(bf16[128,8192]{1,0:T(8,128)(2,1)S(1)} %copy-done, bf16[512,8192]{1,0:T(8,128)(2,1)} %all-gather.9.cloned.1.call-done), kind=kOutput, calls=%fused_computation.4 | convolution fusion | flops 1073807360 | bytes 10616832 | tf_op jit(solution)/shard_map/dot_general | solution.py:102
  (33 shorter events, 0.5 us)
Async XLA Ops:
  7.2 59.2 %copy-start.2 = (s32[128]{0:T(128)S(1)}, s32[128]{0:T(128)}, u32[]{:S(2)}) copy-start(s32[128]{0:T(128)} %param.10) | copy-start | bytes 1540
  7.2 27.0 %copy-start.3 = (s32[128]{0:T(128)S(1)}, s32[128]{0:T(128)}, u32[]{:S(2)}) copy-start(s32[128]{0:T(128)} %param.9) | copy-start | bytes 1540
  7.2 61.1 %copy-start.1 = (bf16[8,8192]{1,0:T(8,128)(2,1)S(1)}, bf16[8,8192]{1,0:T(8,128)(2,1)}, u32[]{:S(2)}) copy-start(bf16[8,8192]{1,0:T(8,128)(2,1)} %param.13) | copy-start | bytes 393220
  11.2 27.4 %all-to-all-start.1 = ((f32[32,1,9]{2,1,0:T(1,128)}), f32[32,1,9]{2,1,0:T(1,128)S(1)}, u32[]{:S(2)}, u32[]{:S(2)}) async-start(f32[32,1,9]{2,1,0:T(1,128)} %broadcast_in_dim.17), calls=%async_computation.1 | async-start | bytes 32768 | tf_op jit(solution)/shard_map/all_to_all | solution.py:14
  27.2 72.7 %all-gather.7.cloned.1.call-start = ((), (), s32[]{:S(2)}) async-start(), calls=%async_computation.5 | async-start | bytes 2359296 | tf_op jit(solution)/shard_map/all_gather | solution.py:65
  39.2 26.8 %all-to-all-start = ((f32[16,3,128]{2,1,0:T(4,128)}), f32[16,3,128]{2,1,0:T(4,128)S(1)}, u32[]{:S(2)}, u32[]{:S(2)}) async-start(f32[16,3,128]{2,1,0:T(4,128)} %broadcast_in_dim.16), calls=%async_computation | async-start | bytes 65536 | tf_op jit(solution)/shard_map/all_to_all | solution.py:14
  51.3 143.1 %all-gather.5.cloned.1.call-start = ((), (), s32[]{:S(2)}) async-start(), calls=%async_computation.4 | async-start | bytes 2228224 | tf_op jit(solution)/shard_map/all_gather | solution.py:101
  69.0 375.2 %all-gather.11.cloned.1.call-start = ((), (), s32[]{:S(2)}) async-start(), calls=%async_computation.7 | async-start | bytes 4325376 | tf_op jit(solution)/shard_map/all_gather | solution.py:110
  69.8 479.9 %all-gather.9.cloned.1.call-start = ((), (), s32[]{:S(2)}) async-start(), calls=%async_computation.6 | async-start | bytes 10485760 | tf_op jit(solution)/shard_map/all_gather | solution.py:65
  101.3 97.2 %all-to-all-start.2 = ((f32[32,1,1]{2,1,0:T(1,128)}), f32[32,1,1]{2,1,0:T(1,128)S(1)}, u32[]{:S(2)}, u32[]{:S(2)}) async-start(f32[32,1,1]{2,1,0:T(1,128)} %broadcast_in_dim.18), calls=%async_computation.2 | async-start | bytes 32768 | tf_op jit(solution)/shard_map/all_to_all | solution.py:14
  198.5 130.9 %all-to-all-start.3 = ((bf16[128,32,256]{0,2,1:T(8,128)(2,1)}), bf16[128,32,256]{0,2,1:T(8,128)(2,1)S(1)}, u32[]{:S(2)}, u32[]{:S(2)}) async-start(bf16[128,32,256]{0,2,1:T(8,128)(2,1)} %bitcast.14), calls=%async_computation.3 | async-start | bytes 4194304 | tf_op jit(solution)/shard_map/all_to_all | solution.py:108
  444.2 105.5 %copy-start = (bf16[128,8192]{1,0:T(8,128)(2,1)S(1)}, bf16[128,8192]{1,0:T(8,128)(2,1)}, u32[]{:S(2)}) copy-start(bf16[128,8192]{1,0:T(8,128)(2,1)} %all-gather.5.cloned.1.call-done) | copy-start | bytes 6291460
Sparse Core Ops, SparseCore 0:
  30.1 69.8 all-gather.6
  103.8 90.5 all-gather.4
  196.5 247.6 all-gather.10
  446.2 103.4 all-gather.8
where the time goes:
time: 564 us; the launch traced here: 563 us
  waiting for transfers between devices  470 us (83%)
  starting transfers between devices  43 us (8%)
  between operations  16.5 us (3%)
  local copies, waits for them, and re-layouts  13 us (2%)
  matrix products  11.2 us (2%)
  other arithmetic  9.9 us (2%)
    all_gather x2, waiting for transfers between devices, whole_of(): shard = lax.all_gather(shard, axis, axis=dim, tiled=True)  131 us
    all_to_all x1, waiting for transfers between devices, shards(): lax.all_to_all(grad_group, DP, split_axis=1, concat_axis=0, tiled=True)  125 us
    all_gather x1, waiting for transfers between devices, shards(): lax.all_gather(mix, DP, axis=0, tiled=True)  112 us
    all_gather x1, waiting for transfers between devices, shards(): grad_group = lax.all_gather(grad_local, 'mp', axis=0, tiled=True)  83.4 us
    all_to_all x3, starting transfers between devices, from_everyone(): lax.all_to_all(jnp.broadcast_to(shard[None], (count, *shard.shape)), axis...  38 us
    all_to_all x3, waiting for transfers between devices, from_everyone(): lax.all_to_all(jnp.broadcast_to(shard[None], (count, *shard.shape)), axis...  17 us
  transfers between devices with their start and end apart: 8, of which 7 were waited for; matrix products, arithmetic and copies ran while one was open for 4% of the time, Pallas kernels for 0%

commit v1 on v0

--- a/solution.py
+++ b/solution.py
@@ -107,7 +107,7 @@
     ).astype(jnp.bfloat16)
     grad_every = lax.all_to_all(grad_group, DP, split_axis=1, concat_axis=0, tiled=True)
     grad_w_out = lax.dot_general(
-        lax.all_gather(mix, DP, axis=0, tiled=True),
+        jnp.concatenate(lax.all_to_all(jnp.stack([mix] * lax.axis_size(DP), 0), DP, 0, 0), 0),
         grad_every,
         (((0,), (0,)), ((), ())),
         preferred_element_type=jnp.float32,

time: 564 us -> 592 us (1.050)
  blocking collectives: 0 us -> 97.5 us
  waiting for transfers between devices: 470 us -> 398 us
    all_gather x2, waiting for transfers between devices: 131 us -> 287 us  [whole_of(): shard = lax.all_gather(shard, axis, axis=dim, tiled=True)]
    all_gather x1 -> x0, waiting for transfers between devices: 112 us -> none  [shards(): lax.all_gather(mix, DP, axis=0, tiled=True)]
    all_to_all x1, waiting for transfers between devices: 125 us -> 17.5 us  [shards(): lax.all_to_all(jnp.stack([mix] * lax.axis_size(DP), 0), DP, 0, 0)]
    all_to_all x0 -> x1, blocking collectives: none -> 97.5 us  [shards(): lax.all_to_all(grad_group, DP, split_axis=1, concat_axis=0, tiled=True)]
    all_gather x1, waiting for transfers between devices: 83.4 us -> 75.8 us  [shards(): grad_group = lax.all_gather(grad_local, 'mp', axis=0, tiled=True)]
  transfers between devices with their start and end apart: 8 -> 7, of which waited for: 7 -> 6; matrix products, arithmetic and copies ran while one was open for 4% -> 3% of each run, Pallas kernels for 0% -> 0%
where the time goes in v1:
time: 592 us; the launch traced here: 591 us
  waiting for transfers between devices  398 us (67%)
  blocking collectives  97.5 us (16%)
  starting transfers between devices  44.4 us (8%)
  between operations  18.3 us (3%)
  local copies, waits for them, and re-layouts  11.7 us (2%)
  matrix products  11 us (2%)
  other arithmetic  10.5 us (2%)
    all_gather x2, waiting for transfers between devices, whole_of(): shard = lax.all_gather(shard, axis, axis=dim, tiled=True)  287 us
    all_to_all x1, blocking collectives, shards(): lax.all_to_all(grad_group, DP, split_axis=1, concat_axis=0, tiled=True)  97.5 us
    all_gather x1, waiting for transfers between devices, shards(): grad_group = lax.all_gather(grad_local, 'mp', axis=0, tiled=True)  75.8 us
    all_to_all x3, starting transfers between devices, from_everyone(): lax.all_to_all(jnp.broadcast_to(shard[None], (count, *shard.shape)), axis...  34.9 us
    all_to_all x1, waiting for transfers between devices, shards(): lax.all_to_all(jnp.stack([mix] * lax.axis_size(DP), 0), DP, 0, 0)  17.5 us
    all_to_all x3, waiting for transfers between devices, from_everyone(): lax.all_to_all(jnp.broadcast_to(shard[None], (count, *shard.shape)), axis...  16.8 us
  transfers between devices with their start and end apart: 7, of which 6 were waited for; matrix products, arithmetic and copies ran while one was open for 3% of the time, Pallas kernels for 0%

profile of v1, /device:TPU:1, one launch (start us, length us, event | category | flops | bytes accessed | tf_op | source)
XLA Modules:
  0.0 590.9 jit_solution(13725907636530914510)
XLA Ops:
  8.0 0.0 copy-start.3
  8.0 0.0 copy-start.2
  9.3 1.3 convert_reduce_fusion
  10.6 0.7 pad_maximum_fusion.1
  11.3 0.6 broadcast_in_dim.17
  11.9 16.1 %all-to-all-start.1 = ((f32[32,1,9]{2,1,0:T(1,128)}), f32[32,1,9]{2,1,0:T(1,128)S(1)}, u32[]{:S(2)}, u32[]{:S(2)}) async-start(f32[32,1,9]{2,1,0:T(1,128)} %broadcast_in_dim.17), calls=%async_computation.1 | async-start | bytes 32768 | tf_op jit(solution)/shard_map/all_to_all | solution.py:14
  28.0 0.7 fusion.15
  28.7 1.4 reduce_max.9
  30.2 2.4 gather_fusion
  32.6 0.7 fusion.14
  33.3 1.7 exponential_reduce_fusion
  35.0 4.3 all-to-all-done.1
  39.3 0.6 broadcast_in_dim.16
  39.9 12.2 %all-to-all-start = ((f32[16,3,128]{2,1,0:T(4,128)}), f32[16,3,128]{2,1,0:T(4,128)S(1)}, u32[]{:S(2)}, u32[]{:S(2)}) async-start(f32[16,3,128]{2,1,0:T(4,128)} %broadcast_in_dim.16), calls=%async_computation | async-start | bytes 65536 | tf_op jit(solution)/shard_map/all_to_all | solution.py:14
  52.1 0.0 all-gather.4.cloned.1.call-start
  52.2 0.1 reduce_sum.56
  52.2 0.6 slice.121
  52.8 0.7 fusion.11
  54.2 12.5 %all-to-all-done = f32[16,3,128]{2,1,0:T(4,128)S(1)} async-done(((f32[16,3,128]{2,1,0:T(4,128)}), f32[16,3,128]{2,1,0:T(4,128)S(1)}, u32[]{:S(2)}, u32[]{:S(2)}) %all-to-all-start) | async-done | bytes 24608 | tf_op jit(solution)/shard_map/all_to_all | solution.py:14
  67.1 0.0 copy-done.3
  67.1 1.8 multiply_reduce_fusion
  68.9 0.1 dynamic-slice_negate_fusion
  68.9 0.0 copy-done.2
  68.9 0.7 multiply_convert_fusion
  69.7 0.0 all-gather.4.cloned.1.call-update
  70.3 0.6 broadcast_in_dim.18
  71.0 6.6 %all-to-all-start.2 = ((f32[32,1,1]{2,1,0:T(1,128)}), f32[32,1,1]{2,1,0:T(1,128)S(1)}, u32[]{:S(2)}, u32[]{:S(2)}) async-start(f32[32,1,1]{2,1,0:T(1,128)} %broadcast_in_dim.18), calls=%async_computation.2 | async-start | bytes 32768 | tf_op jit(solution)/shard_map/all_to_all | solution.py:14
  77.6 75.8 %all-gather.4.cloned.1.call-done = bf16[128,8192]{1,0:T(8,128)(2,1)} async-done(((bf16[8,8192]{1,0:T(8,128)(2,1)}), bf16[128,8192]{1,0:T(8,128)(2,1)}) %all-gather.4.cloned.1.call-update) | async-done | bytes 2097168 | tf_op jit(solution)/shard_map/all_gather | solution.py:101
  153.3 3.2 copy.34
  156.6 0.0 all-to-all-done.2
  156.6 0.0 copy-start.1
  156.6 97.5 %all_to_all.38 = bf16[128,32,256]{0,2,1:T(8,128)(2,1)} all-to-all(bf16[128,32,256]{0,2,1:T(8,128)(2,1)S(1)} %bitcast.48), channel_id=1, replica_groups=mesh['dp_0'=4,'dp_1'=8,'mp'=16] {'dp_0','dp_1'}, dimensions={1} | all-to-all | bytes 4194304 | tf_op jit(solution)/shard_map/all_to_all | solution.py:108
  254.1 0.0 copy-done.1
  254.1 2.4 stack.2
  256.5 9.4 %all-to-all-start.4 = ((bf16[32,128,512]{2,1,0:T(8,128)(2,1)}), bf16[32,128,512]{2,1,0:T(8,128)(2,1)}, u32[]{:S(2)}, u32[]{:S(2)}) async-start(bf16[32,128,512]{2,1,0:T(8,128)(2,1)} %stack.2), calls=%async_computation.4 | async-start | bytes 8388608 | tf_op jit(solution)/shard_map/all_to_all | solution.py:110
  265.9 0.0 all-gather.6.cloned.1.call-start
  266.0 0.5 all-gather.6.cloned.1.call-update
  266.5 0.0 all-gather.8.cloned.1.call-start
  266.6 197.7 %all-gather.6.cloned.1.call-done = bf16[512,2048]{1,0:T(8,128)(2,1)} async-done(((bf16[512,256]{1,0:T(8,128)(2,1)}), bf16[512,2048]{1,0:T(8,128)(2,1)}) %all-gather.6.cloned.1.call-update) | async-done | bytes 2097168 | tf_op jit(solution)/shard_map/all_gather | solution.py:65
  464.2 0.0 all-gather.8.cloned.1.call-update
  464.3 0.6 reduce_sum.59
  464.9 0.0 copy-start
  464.9 17.5 %all-to-all-done.4 = bf16[32,128,512]{2,1,0:T(8,128)(2,1)} async-done(((bf16[32,128,512]{2,1,0:T(8,128)(2,1)}), bf16[32,128,512]{2,1,0:T(8,128)(2,1)}, u32[]{:S(2)}, u32[]{:S(2)}) %all-to-all-start.4) | async-done | bytes 4194336 | tf_op jit(solution)/shard_map/all_to_all | solution.py:110
  482.4 4.1 fusion.8
  486.4 0.8 copy.35
  487.3 89.3 %all-gather.8.cloned.1.call-done = bf16[512,8192]{1,0:T(8,128)(2,1)} async-done(((bf16[512,2048]{1,0:T(8,128)(2,1)}), bf16[512,8192]{1,0:T(8,128)(2,1)}) %all-gather.8.cloned.1.call-update) | async-done | bytes 8388624 | tf_op jit(solution)/shard_map/all_gather | solution.py:65
  576.5 0.0 copy-done
  576.5 7.0 %convolution_convert_fusion = bf16[128,512]{1,0:T(8,128)(2,1)} fusion(bf16[128,8192]{1,0:T(8,128)(2,1)S(1)} %copy-done, bf16[512,8192]{1,0:T(8,128)(2,1)} %all-gather.8.cloned.1.call-done), kind=kOutput, calls=%fused_computation.7 | convolution fusion | flops 1073807360 | bytes 10616832 | tf_op jit(solution)/shard_map/dot_general | solution.py:102
  (31 shorter events, 0.4 us)
Async XLA Ops:
  8.0 59.1 %copy-start.3 = (s32[128]{0:T(128)S(1)}, s32[128]{0:T(128)}, u32[]{:S(2)}) copy-start(s32[128]{0:T(128)} %param.10) | copy-start | bytes 1540
  8.0 60.9 %copy-start.2 = (bf16[8,8192]{1,0:T(8,128)(2,1)S(1)}, bf16[8,8192]{1,0:T(8,128)(2,1)}, u32[]{:S(2)}) copy-start(bf16[8,8192]{1,0:T(8,128)(2,1)} %param.13) | copy-start | bytes 393220
  11.9 27.4 %all-to-all-start.1 = ((f32[32,1,9]{2,1,0:T(1,128)}), f32[32,1,9]{2,1,0:T(1,128)S(1)}, u32[]{:S(2)}, u32[]{:S(2)}) async-start(f32[32,1,9]{2,1,0:T(1,128)} %broadcast_in_dim.17), calls=%async_computation.1 | async-start | bytes 32768 | tf_op jit(solution)/shard_map/all_to_all | solution.py:14
  39.9 26.7 %all-to-all-start = ((f32[16,3,128]{2,1,0:T(4,128)}), f32[16,3,128]{2,1,0:T(4,128)S(1)}, u32[]{:S(2)}, u32[]{:S(2)}) async-start(f32[16,3,128]{2,1,0:T(4,128)} %broadcast_in_dim.16), calls=%async_computation | async-start | bytes 65536 | tf_op jit(solution)/shard_map/all_to_all | solution.py:14
  52.1 101.2 %all-gather.4.cloned.1.call-start = ((), (), s32[]{:S(2)}) async-start(), calls=%async_computation.5 | async-start | bytes 2228224 | tf_op jit(solution)/shard_map/all_gather | solution.py:101
  71.0 85.6 %all-to-all-start.2 = ((f32[32,1,1]{2,1,0:T(1,128)}), f32[32,1,1]{2,1,0:T(1,128)S(1)}, u32[]{:S(2)}, u32[]{:S(2)}) async-start(f32[32,1,1]{2,1,0:T(1,128)} %broadcast_in_dim.18), calls=%async_computation.2 | async-start | bytes 32768 | tf_op jit(solution)/shard_map/all_to_all | solution.py:14
  156.6 97.5 %copy-start.1 = (bf16[128,512]{1,0:T(8,128)(2,1)S(1)}, bf16[128,512]{1,0:T(8,128)(2,1)}, u32[]{:S(2)}) copy-start(bf16[128,512]{1,0:T(8,128)(2,1)} %param.14) | copy-start | bytes 393220
  256.5 225.9 %all-to-all-start.4 = ((bf16[32,128,512]{2,1,0:T(8,128)(2,1)}), bf16[32,128,512]{2,1,0:T(8,128)(2,1)}, u32[]{:S(2)}, u32[]{:S(2)}) async-start(bf16[32,128,512]{2,1,0:T(8,128)(2,1)} %stack.2), calls=%async_computation.4 | async-start | bytes 8388608 | tf_op jit(solution)/shard_map/all_to_all | solution.py:110
  265.9 198.3 %all-gather.6.cloned.1.call-start = ((), (), s32[]{:S(2)}) async-start(), calls=%async_computation.6 | async-start | bytes 2359296 | tf_op jit(solution)/shard_map/all_gather | solution.py:65
  266.5 310.0 %all-gather.8.cloned.1.call-start = ((), (), s32[]{:S(2)}) async-start(), calls=%async_computation.7 | async-start | bytes 10485760 | tf_op jit(solution)/shard_map/all_gather | solution.py:65
  464.9 111.6 %copy-start = (bf16[128,8192]{1,0:T(8,128)(2,1)S(1)}, bf16[128,8192]{1,0:T(8,128)(2,1)}, u32[]{:S(2)}) copy-start(bf16[128,8192]{1,0:T(8,128)(2,1)} %all-gather.4.cloned.1.call-done) | copy-start | bytes 6291460
Sparse Core Ops, SparseCore 0:
  69.8 83.4 all-gather.3
Sparse Core Ops, SparseCore 1:
  268.4 195.8 all-gather.5
  466.2 110.3 all-gather.7
